TPU v7x, 32 devices: a whole 2x2x4 slice. The times are simulated.
32 devices in a mesh: dof: 8 (over y, x, core), tm: 4 (over z).
Axes of the slice: x: 2, y: 2, z: 4, core: 2. Of those that a mesh axis runs over, the one named last changes fastest.
Arguments:
- snapshots: bfloat16 [163840, 1024], P('dof', 'tm'), may hold values from -6 to 6
- basis: bfloat16 [163840, 64], P('dof'), may hold values from -0.015625 to 0.015625
Outputs:
- gram: float32 [2144, 2144], P('tm', 'dof')
- coords: float32 [64, 1024], P(None, 'tm')
All inputs are finite; a program needn't handle non-finite values.
Results may differ from a plain program's by a relative error of at most 0.0021.
Values may be sent and summed in bfloat16 or wider, within the bound.
No kernel may reach another device: no remote copies, remote signals or barrier semaphores. Data moves between devices by JAX's collectives and lax.ppermute only.
A program may use at most 64 MiB of HBM per device.

v0:
```python
import jax
import jax.numpy as jnp
import numpy as np
from jax import lax
from jax.sharding import PartitionSpec as P


def build_features(coords):
    modes = coords.shape[0]
    upper_i, upper_j = np.triu_indices(modes)
    quad = coords[upper_i, :] * coords[upper_j, :]
    return jnp.concatenate([coords, quad], axis=0).astype(jnp.bfloat16)


def on_device(snapshots, basis):
    partial_proj = lax.dot_general(
        basis, snapshots, (((0,), (0,)), ((), ())), preferred_element_type=jnp.float32
    )
    coords = lax.psum(partial_proj, "dof")
    features = build_features(coords)
    feature_count = features.shape[0]
    inverse_total = 1.0 / (features.shape[1] * lax.axis_size("tm"))
    owned_rows = feature_count // lax.axis_size("tm")
    col_width = feature_count // lax.axis_size("dof")
    col_start = lax.axis_index("dof") * col_width
    row_start = lax.axis_index("tm") * owned_rows
    initial = jnp.zeros((owned_rows, col_width), jnp.float32)
    piece = lax.all_gather(features, "tm", axis=1, tiled=True)
    row_part = lax.dynamic_slice_in_dim(piece, row_start, owned_rows, 0)
    col_part = lax.dynamic_slice_in_dim(piece, col_start, col_width, 0)
    product = lax.dot_general(
        row_part, col_part, (((1,), (1,)), ((), ())), preferred_element_type=jnp.float32
    )
    gram = initial + product * inverse_total
    return (gram, coords)


def solution(mesh):
    placed = (P("dof", "tm"), P("dof", None))
    return jax.shard_map(
        on_device,
        mesh=mesh,
        in_specs=placed,
        out_specs=(P("tm", "dof"), P(None, "tm")),
        check_vma=False,
    )
```

profile of v0, /device:TPU:0, one launch (start us, length us, event | category | flops | bytes accessed | tf_op | source)
XLA Modules:
  0.0 182.3 jit_solution(5816619657642350401)
XLA Ops:
  7.2 0.0 copy-start
  7.2 0.0 copy-start.2
  7.2 0.0 copy-start.3
  7.2 0.0 all-reduce.2.cloned.1.call-start
  7.2 1.7 copy-done
  8.9 6.4 %fusion.3 = f32[64,256]{1,0:T(8,128)} fusion(bf16[20480,64]{0,1:T(8,128)(2,1)S(1)} %copy-done, bf16[20480,256]{1,0:T(8,128)(2,1)} %param.6), kind=kOutput, calls=%fused_computation.10 | convolution fusion | flops 671088640 | bytes 13172736 | tf_op jit(solution)/shard_map/dot_general | solution.py:16
  15.3 0.0 all-reduce.2.cloned.1.call-update
  15.4 0.0 all-gather.2.cloned.1.call-start
  15.4 0.0 copy-done.2
  15.4 0.0 copy-done.3
  15.4 56.0 %all-reduce.2.cloned.1.call-done = f32[64,256]{1,0:T(8,128)} async-done(((f32[64,256]{1,0:T(8,128)}), f32[64,256]{1,0:T(8,128)}) %all-reduce.2.cloned.1.call-update) | async-done | bytes 65552 | tf_op jit(solution)/shard_map/psum | solution.py:19
  71.4 0.0 copy-start.1
  71.4 7.3 %gather_fusion = f32[2080,256]{1,0:T(8,128)} fusion(f32[64,256]{1,0:T(8,128)} %all-reduce.2.cloned.1.call-done, s32[3072]{0:T(1024)S(1)} %pad_clamp_fusion.1), kind=kCustom, calls=%fused_computation | custom fusion | bytes 4268160 | tf_op jit(solution)/shard_map/gather | solution.py:11
  78.7 0.0 copy-done.1
  78.7 6.4 %gather_fusion.1 = f32[2080,256]{1,0:T(8,128)} fusion(f32[64,256]{1,0:T(8,128)S(1)} %copy-done.1, s32[3072]{0:T(1024)S(1)} %pad_clamp_fusion), kind=kCustom, calls=%fused_computation.1 | custom fusion | bytes 4268160 | tf_op jit(solution)/shard_map/gather | solution.py:11
  85.0 2.5 %multiply_convert_fusion = bf16[2080,256]{1,0:T(8,128)(2,1)S(1)} fusion(f32[2080,256]{1,0:T(8,128)} %gather_fusion, f32[2080,256]{1,0:T(8,128)} %gather_fusion.1), kind=kLoop, calls=%fused_computation.2 | loop fusion | flops 1064960 | bytes 5324800 | tf_op jit(solution)/shard_map/convert.1
  87.5 1.1 pad_maximum_fusion
  88.6 0.0 all-gather.2.cloned.1.call-update
  88.6 83.3 %all-gather.2.cloned.1.call-done = bf16[2144,1024]{1,0:T(8,128)(2,1)} async-done(((bf16[2144,256]{1,0:T(8,128)(2,1)}), bf16[2144,1024]{1,0:T(8,128)(2,1)}) %all-gather.2.cloned.1.call-update) | async-done | bytes 4390928 | tf_op jit(solution)/shard_map/all_gather | solution.py:28
  171.9 2.9 %convolution_multiply_fusion = f32[536,268]{0,1:T(8,128)} fusion(bf16[2144,1024]{1,0:T(8,128)(2,1)} %all-gather.2.cloned.1.call-done, s32[]{:T(128)S(6)} %select_n.14, s32[]{:T(128)S(6)} %select_n.15), kind=kOutput, calls=%fused_computation.3 | convolution fusion | flops 294334752 | bytes 2229384 | tf_op jit(solution)/shard_map/dot_general | solution.py:31
  174.8 0.6 copy.9
  (3 shorter events, 0.0 us)
Async XLA Ops:
  7.2 1.7 copy-start
  7.2 8.2 %copy-start.2 = (s32[2080]{0:T(1024)S(1)}, s32[2080]{0:T(1024)}, u32[]{:S(2)}) copy-start(s32[2080]{0:T(1024)} %constant.32) | copy-start | bytes 24964
  7.2 8.2 %copy-start.3 = (s32[2080]{0:T(1024)S(1)}, s32[2080]{0:T(1024)}, u32[]{:S(2)}) copy-start(s32[2080]{0:T(1024)} %constant.33) | copy-start | bytes 24964
  7.2 64.2 %all-reduce.2.cloned.1.call-start = ((), (), s32[]{:S(2)}) async-start(), calls=%async_computation | async-start | bytes 131072 | tf_op jit(solution)/shard_map/psum | solution.py:19
  15.4 156.6 %all-gather.2.cloned.1.call-start = ((), (), s32[]{:S(2)}) async-start(), calls=%async_computation.1 | async-start | bytes 5488640 | tf_op jit(solution)/shard_map/all_gather | solution.py:28
  71.4 7.3 %copy-start.1 = (f32[64,256]{1,0:T(8,128)S(1)}, f32[64,256]{1,0:T(8,128)}, u32[]{:S(2)}) copy-start(f32[64,256]{1,0:T(8,128)} %all-reduce.2.cloned.1.call-done) | copy-start | bytes 196612
Sparse Core Ops, SparseCore 0:
  15.5 55.8 all-reduce.1
  88.7 83.1 all-gather.1
where the time goes:
time: 183 us; the launch traced here: 182 us
  waiting for transfers between devices  139 us (76%)
  local copies, waits for them, and re-layouts  15.9 us (9%)
  between operations  14.1 us (8%)
  matrix products  9.32 us (5%)
  other arithmetic  3.55 us (2%)
    all_gather x1, waiting for transfers between devices, on_device(): piece = lax.all_gather(features, 'tm', axis=1, tiled=True)  83.3 us
    psum x1, waiting for transfers between devices, on_device(): coords = lax.psum(partial_proj, 'dof')  56 us
    gather x2, local copies, waits for them, and re-layouts, build_features(): quad = coords[upper_i, :] * coords[upper_j, :]  13.6 us
    dot_general x1, matrix products, on_device(): lax.dot_general(basis, snapshots, (((0,), (0,)), ((), ())), preferred_ele...  6.42 us
  transfers between devices with their start and end apart: 2, of which 2 were waited for; matrix products, arithmetic and copies ran while one was open for 0% of the time, Pallas kernels for 0%

commit v1 on v0

--- a/solution.py
+++ b/solution.py
@@ -16,7 +16,9 @@
     partial_proj = lax.dot_general(
         basis, snapshots, (((0,), (0,)), ((), ())), preferred_element_type=jnp.float32
     )
-    coords = lax.psum(partial_proj, "dof")
+    coords = partial_proj
+    for hop in (1, 2, 4):
+        coords = coords + lax.ppermute(coords, "dof", [(dev, dev ^ hop) for dev in range(8)])
     features = build_features(coords)
     feature_count = features.shape[0]
     inverse_total = 1.0 / (features.shape[1] * lax.axis_size("tm"))

time: 183 us -> 138 us (0.75)
  waiting for transfers between devices: 139 us -> 91.2 us
  starting transfers between devices: 0.08 us -> 5.43 us
    psum x1 -> x0, waiting for transfers between devices: 56 us -> none  [on_device(): coords = lax.psum(partial_proj, 'dof')]
    ppermute x0 -> x3, waiting for transfers between devices: none -> 5.68 us  [on_device(): lax.ppermute(coords, 'dof', [(dev, dev ^ hop) for dev in range(8)])]
    ppermute x0 -> x3, starting transfers between devices: none -> 5.4 us  [on_device(): lax.ppermute(coords, 'dof', [(dev, dev ^ hop) for dev in range(8)])]
    all_gather x1, waiting for transfers between devices: 83.3 us -> 85.5 us  [on_device(): piece = lax.all_gather(features, 'tm', axis=1, tiled=True)]
  transfers between devices with their start and end apart: 2 -> 4, of which waited for: 2 -> 4; matrix products, arithmetic and copies ran while one was open for 0% -> 0% of each run, Pallas kernels for 0% -> 0%
where the time goes in v1:
time: 138 us; the launch traced here: 137 us
  waiting for transfers between devices  91.2 us (66%)
  local copies, waits for them, and re-layouts  14.5 us (11%)
  between operations  14.1 us (10%)
  matrix products  8.67 us (6%)
  starting transfers between devices  5.43 us (4%)
  other arithmetic  3.59 us (3%)
    all_gather x1, waiting for transfers between devices, on_device(): piece = lax.all_gather(features, 'tm', axis=1, tiled=True)  85.5 us
    gather x2, local copies, waits for them, and re-layouts, build_features(): quad = coords[upper_i, :] * coords[upper_j, :]  12.8 us
    dot_general x1, matrix products, on_device(): lax.dot_general(basis, snapshots, (((0,), (0,)), ((), ())), preferred_ele...  5.78 us
    ppermute x3, waiting for transfers between devices, on_device(): lax.ppermute(coords, 'dof', [(dev, dev ^ hop) for dev in range(8)])  5.68 us
    ppermute x3, starting transfers between devices, on_device(): lax.ppermute(coords, 'dof', [(dev, dev ^ hop) for dev in range(8)])  5.4 us
    dot_general x1, matrix products, on_device(): lax.dot_general(row_part, col_part, (((1,), (1,)), ((), ())), preferred_e...  2.89 us
  transfers between devices with their start and end apart: 4, of which 4 were waited for; matrix products, arithmetic and copies ran while one was open for 0% of the time, Pallas kernels for 0%

profile of v1, /device:TPU:0, one launch (start us, length us, event | category | flops | bytes accessed | tf_op | source)
XLA Modules:
  0.0 137.5 jit_solution(13661420188457261264)
XLA Ops:
  7.2 0.0 copy-start
  7.2 0.0 copy-start.3
  7.2 0.0 copy-start.2
  7.2 0.0 all-gather.2.cloned.1.call-start
  7.2 1.7 %copy-done = bf16[20480,64]{0,1:T(8,128)(2,1)S(1)} copy-done((bf16[20480,64]{0,1:T(8,128)(2,1)S(1)}, bf16[20480,64]{0,1:T(8,128)(2,1)}, u32[]{:S(2)}) %copy-start) | copy-done | bytes 2621464
  8.9 5.8 %fusion.4 = f32[64,256]{1,0:T(8,128)S(1)} fusion(bf16[20480,64]{0,1:T(8,128)(2,1)S(1)} %copy-done, bf16[20480,256]{1,0:T(8,128)(2,1)} %param.6), kind=kOutput, calls=%fused_computation.11 | convolution fusion | flops 671088640 | bytes 13172736 | tf_op jit(solution)/shard_map/dot_general | solution.py:16
  14.7 0.6 collective-permute-start
  15.3 0.9 collective-permute-done
  16.2 2.9 %collective-permute-start.1 = (f32[64,256]{1,0:T(8,128)S(1)}, f32[64,256]{1,0:T(8,128)S(1)}, u32[]{:S(2)}, u32[]{:S(2)}) collective-permute-start(f32[64,256]{1,0:T(8,128)S(1)} %add.21), channel_id=1, source_target_pairs={{0,8},{4,12},{8,0},{12,4},{16,24},{20,28},{24,16},{28,20},{1,9},{5... | collective-permute-start | bytes 196616 | tf_op jit(solution)/shard_map/ppermute | solution.py:21
  19.1 0.0 copy-done.3
  19.1 2.4 %collective-permute-done.1 = f32[64,256]{1,0:T(8,128)S(1)} collective-permute-done((f32[64,256]{1,0:T(8,128)S(1)}, f32[64,256]{1,0:T(8,128)S(1)}, u32[]{:S(2)}, u32[]{:S(2)}) %collective-permute-start.1) | collective-permute-done | bytes 65568 | tf_op jit(solution)/shard_map/ppermute | solution.py:21
  21.5 1.9 %collective-permute-start.2 = (f32[64,256]{1,0:T(8,128)S(1)}, f32[64,256]{1,0:T(8,128)S(1)}, u32[]{:S(2)}, u32[]{:S(2)}) collective-permute-start(f32[64,256]{1,0:T(8,128)S(1)} %add.22), channel_id=1, source_target_pairs={{0,16},{4,20},{8,24},{12,28},{16,0},{20,4},{24,8},{28,12},{1,17},{... | collective-permute-start | bytes 196616 | tf_op jit(solution)/shard_map/ppermute | solution.py:21
  23.4 0.0 copy-done.2
  23.5 2.4 %collective-permute-done.2 = f32[64,256]{1,0:T(8,128)S(1)} collective-permute-done((f32[64,256]{1,0:T(8,128)S(1)}, f32[64,256]{1,0:T(8,128)S(1)}, u32[]{:S(2)}, u32[]{:S(2)}) %collective-permute-start.2) | collective-permute-done | bytes 65568 | tf_op jit(solution)/shard_map/ppermute | solution.py:21
  25.8 0.0 copy-start.1
  25.9 6.4 %gather_fusion = f32[2080,256]{1,0:T(8,128)} fusion(f32[64,256]{1,0:T(8,128)S(1)} %get-tuple-element.3, s32[3072]{0:T(1024)S(1)} %pad_clamp_fusion.1), kind=kCustom, calls=%fused_computation | custom fusion | bytes 4268160 | tf_op jit(solution)/shard_map/gather | solution.py:11
  32.3 0.0 copy-done.1
  32.3 6.4 %gather_fusion.1 = f32[2080,256]{1,0:T(8,128)} fusion(f32[64,256]{1,0:T(8,128)S(1)} %get-tuple-element.3, s32[3072]{0:T(1024)S(1)} %pad_clamp_fusion), kind=kCustom, calls=%fused_computation.1 | custom fusion | bytes 4268160 | tf_op jit(solution)/shard_map/gather | solution.py:11
  38.7 2.5 %multiply_convert_fusion = bf16[2080,256]{1,0:T(8,128)(2,1)S(1)} fusion(f32[2080,256]{1,0:T(8,128)} %gather_fusion, f32[2080,256]{1,0:T(8,128)} %gather_fusion.1), kind=kLoop, calls=%fused_computation.2 | loop fusion | flops 1064960 | bytes 5324800 | tf_op jit(solution)/shard_map/convert.1
  41.1 1.1 pad_maximum_fusion
  42.2 0.0 all-gather.2.cloned.1.call-update
  42.2 85.5 %all-gather.2.cloned.1.call-done = bf16[2144,1024]{1,0:T(8,128)(2,1)} async-done(((bf16[2144,256]{1,0:T(8,128)(2,1)}), bf16[2144,1024]{1,0:T(8,128)(2,1)}) %all-gather.2.cloned.1.call-update) | async-done | bytes 4390928 | tf_op jit(solution)/shard_map/all_gather | solution.py:30
  127.8 2.9 %convolution_multiply_fusion = f32[536,268]{0,1:T(8,128)} fusion(bf16[2144,1024]{1,0:T(8,128)(2,1)} %all-gather.2.cloned.1.call-done, s32[]{:T(128)S(6)} %select_n.14, s32[]{:T(128)S(6)} %select_n.15), kind=kOutput, calls=%fused_computation.3 | convolution fusion | flops 294334752 | bytes 2229384 | tf_op jit(solution)/shard_map/dot_general | solution.py:33
  (5 shorter events, 0.0 us)
Async XLA Ops:
  7.2 1.7 %copy-start = (bf16[20480,64]{0,1:T(8,128)(2,1)S(1)}, bf16[20480,64]{0,1:T(8,128)(2,1)}, u32[]{:S(2)}) copy-start(bf16[20480,64]{0,1:T(8,128)(2,1)} %param.7) | copy-start | bytes 7864324
  7.2 11.9 %copy-start.3 = (s32[2080]{0:T(1024)S(1)}, s32[2080]{0:T(1024)}, u32[]{:S(2)}) copy-start(s32[2080]{0:T(1024)} %constant.32) | copy-start | bytes 24964
  7.2 16.3 %copy-start.2 = (s32[2080]{0:T(1024)S(1)}, s32[2080]{0:T(1024)}, u32[]{:S(2)}) copy-start(s32[2080]{0:T(1024)} %constant.33) | copy-start | bytes 24964
  7.2 120.6 %all-gather.2.cloned.1.call-start = ((), (), s32[]{:S(2)}) async-start(), calls=%async_computation | async-start | bytes 5488640 | tf_op jit(solution)/shard_map/all_gather | solution.py:30
  14.7 1.5 %collective-permute-start = (f32[64,256]{1,0:T(8,128)S(1)}, f32[64,256]{1,0:T(8,128)S(1)}, u32[]{:S(2)}, u32[]{:S(2)}) collective-permute-start(f32[64,256]{1,0:T(8,128)S(1)} %fusion.4), channel_id=1, source_target_pairs={{0,4},{4,0},{8,12},{12,8},{16,20},{20,16},{24,28},{28,24},{1,5},{5... | collective-permute-start | bytes 196616 | tf_op jit(solution)/shard_map/ppermute | solution.py:21
  16.2 5.3 %collective-permute-start.1 = (f32[64,256]{1,0:T(8,128)S(1)}, f32[64,256]{1,0:T(8,128)S(1)}, u32[]{:S(2)}, u32[]{:S(2)}) collective-permute-start(f32[64,256]{1,0:T(8,128)S(1)} %add.21), channel_id=1, source_target_pairs={{0,8},{4,12},{8,0},{12,4},{16,24},{20,28},{24,16},{28,20},{1,9},{5... | collective-permute-start | bytes 196616 | tf_op jit(solution)/shard_map/ppermute | solution.py:21
  21.5 4.3 %collective-permute-start.2 = (f32[64,256]{1,0:T(8,128)S(1)}, f32[64,256]{1,0:T(8,128)S(1)}, u32[]{:S(2)}, u32[]{:S(2)}) collective-permute-start(f32[64,256]{1,0:T(8,128)S(1)} %add.22), channel_id=1, source_target_pairs={{0,16},{4,20},{8,24},{12,28},{16,0},{20,4},{24,8},{28,12},{1,17},{... | collective-permute-start | bytes 196616 | tf_op jit(solution)/shard_map/ppermute | solution.py:21
  25.8 6.4 %copy-start.1 = (f32[64,256]{1,0:T(8,128)}, f32[64,256]{1,0:T(8,128)S(1)}, u32[]{:S(2)}) copy-start(f32[64,256]{1,0:T(8,128)S(1)} %get-tuple-element.3) | copy-start | bytes 196612
Sparse Core Ops, SparseCore 0:
  42.4 85.3 all-gather.1
